TPU v7x, 256 devices: a 4x2x16 block of a 4x16x16 slice. The times are simulated.
256 devices in a mesh: cfg: 2 (over y), space: 16 (over z), tm: 8 (over x, core).
Axes of the slice: x: 4, y: 2, z: 16, core: 2. Of those that a mesh axis runs over, the one named last changes fastest.
The devices are a block of a 4x16x16 slice.
Arguments:
- solutions: bfloat16 [32, 128, 32, 12288], P(('cfg', 'tm'), None, None, 'space'), parts along dimension 0, may hold values from -6 to 6
- eigvecs: bfloat16 [32, 2, 128, 12288], P(('cfg', 'tm'), None, 'space'), parts along dimension 0, may hold values from -0.0390625 to 0.0390625
- source_time: int32 [256], P('cfg'), parts along dimension 0, may hold values from 0 to 15
Outputs:
- perambulator: bfloat16 [32, 128, 32, 128], P(('cfg', 'tm'), 'space'), parts along dimension 0
There are 2 independent parts, one for each index of `cfg`. A program takes and returns all parts, laid end to end along the dimension named above; each array names one. Nothing has to cross between parts.
All inputs are finite; a program needn't handle non-finite values.
Results may differ from a plain program's by a relative error of at most 0.001.
Values may be sent and summed in bfloat16 or wider, within the bound.
No kernel may reach another device: no remote copies, remote signals or barrier semaphores. Data moves between devices by JAX's collectives and lax.ppermute only.
A program may use at most 128 MiB of HBM per device.

v0:
```python
import jax
import jax.numpy as jnp
from jax import lax
from jax.sharding import PartitionSpec as P


def cut_along(array, dim, peers):
    lengths = array.shape
    parts = array.reshape(*lengths[:dim], peers, lengths[dim] // peers, *lengths[dim + 1 :])
    return jnp.moveaxis(parts, dim, 0)


def edges_of(length, count):
    unit = 8 if length >= 8 * count else 1
    return [length // unit * k // count * unit for k in range(1, count)]


def in_order(parts, dim):
    lengths = list(parts.shape[1:])
    lengths[dim] *= parts.shape[0]
    return jnp.moveaxis(parts, 0, dim).reshape(lengths)


def several_exchanges(array, axis, pieces, split_dim, concat_dim):
    parts = cut_along(array, split_dim, lax.axis_size(axis))
    split_at = max(range(1, max(2, parts.ndim - 1)), key=lambda d: parts.shape[d])
    done = []
    for section in jnp.split(parts, edges_of(parts.shape[split_at], pieces), axis=split_at):
        if section.size:
            done.append(lax.all_to_all(section, axis, split_axis=0, concat_axis=0, tiled=True))
    return in_order(jnp.concatenate(done, axis=split_at), concat_dim)


def contract_block(spinors, vectors):
    slices = spinors.shape[0]
    sources = spinors.shape[1]
    count = vectors.shape[2]
    stacked = vectors.reshape(slices, 2 * count, vectors.shape[3])
    products = jnp.einsum(
        "tkc,tjc->tkj",
        spinors.reshape(slices, sources * 32, spinors.shape[3]),
        stacked,
        preferred_element_type=jnp.float32,
    )
    products = products.reshape(slices, sources, 2, 16, 2, count)
    real_part = products[:, :, 0, :, 0, :] + products[:, :, 1, :, 1, :]
    imag_part = products[:, :, 1, :, 0, :] - products[:, :, 0, :, 1, :]
    return jnp.concatenate([real_part, imag_part], axis=2)


def shards(solutions, eigvecs, source_time):
    slices = solutions.shape[0]
    local_vectors = several_exchanges(eigvecs, "space", 2, 3, 2)
    partial_value = contract_block(solutions, local_vectors)
    sums = lax.psum_scatter(partial_value, "space", scatter_dimension=1, tiled=True)
    owned = sums.shape[1]
    first_source = lax.axis_index("space") * owned
    owned_times = lax.dynamic_slice_in_dim(source_time, first_source, owned)
    slice_index = lax.axis_index("tm") * slices + jnp.arange(slices, dtype=jnp.int32)
    signs = jnp.where(slice_index[:, None] < owned_times[None, :], -1.0, 1.0).astype(jnp.float32)
    return (sums * signs[:, :, None, None]).astype(jnp.bfloat16)


def solution(mesh):
    return jax.shard_map(
        shards,
        mesh=mesh,
        in_specs=(
            P(("cfg", "tm"), None, None, "space"),
            P(("cfg", "tm"), None, "space", None),
            P("cfg"),
        ),
        out_specs=P(("cfg", "tm"), "space", None, None),
        check_vma=False,
    )
```

profile of v0, /device:TPU:34, one launch (start us, length us, event | category | flops | bytes accessed | tf_op | source)
XLA Modules:
  0.0 222.1 jit_solution(175598920798950738)
XLA Ops:
  6.5 1.3 copy.25
  7.8 0.1 fusion.2
  7.9 0.9 copy.15
  8.8 24.0 %all-to-all-start = ((bf16[16,2,2,4,768]{4,3,2,1,0:T(4,128)(2,1)}), bf16[16,2,2,4,768]{4,3,2,1,0:T(4,128)(2,1)S(1)}, u32[]{:S(2)}, u32[]{:S(2)}) async-start(bf16[16,2,2,4,768]{4,3,2,1,0:T(4,128)(2,1)} %copy.15), calls=%async_computation | async-start | bytes 786432 | tf_op jit(solution)/shard_map/all_to_all | solution.py:30
  32.8 0.1 reduce-scatter.5.cloned.1.call-start
  32.9 0.2 copy.16
  33.1 23.4 %all-to-all-done = bf16[16,2,2,4,768]{4,3,2,1,0:T(4,128)(2,1)S(1)} async-done(((bf16[16,2,2,4,768]{4,3,2,1,0:T(4,128)(2,1)}), bf16[16,2,2,4,768]{4,3,2,1,0:T(4,128)(2,1)S(1)}, u32[]{:S(2)}, u32[]{:S(2)}) %all-to-all-start) | async-done | bytes 393248 | tf_op jit(solution)/shard_map/all_to_all | solution.py:30
  56.5 29.5 %all_to_all.10 = bf16[16,2,2,4,768]{4,3,2,1,0:T(4,128)(2,1)S(1)} all-to-all(bf16[16,2,2,4,768]{4,3,2,1,0:T(4,128)(2,1)S(1)} %copy.16), channel_id=1, replica_groups=mesh['cfg'=2,'space'=16,'tm'=8] {'space'}, dimensions={0} | all-to-all | bytes 786432 | tf_op jit(solution)/shard_map/all_to_all | solution.py:30
  86.1 0.4 maximum_bitcast_fusion
  86.5 0.1 copy.17
  86.5 14.7 %convolution_bitcast_fusion = f32[2,4096,256]{1,2,0:T(8,128)} fusion(bf16[2,256,768]{2,1,0:T(8,128)(2,1)S(1)} %bitcast.40, bf16[2,4096,768]{2,1,0:T(8,128)(2,1)} %bitcast.35), kind=kOutput, calls=%fused_computation | convolution fusion | flops 3221225472 | bytes 21757952 | tf_op jit(solution)/shard_map/tkc,tjc->tkj/dot_general | solution.py:39
  101.2 8.9 %copy.18 = f32[2,4096,256]{2,1,0:T(8,128)} copy(f32[2,4096,256]{1,2,0:T(8,128)} %convolution_bitcast_fusion) | data formatting | bytes 16777216 | tf_op jit(solution)/shard_map/tkc,tjc->tkj/dot_general | solution.py:39
  110.1 10.8 %reshape.44 = f32[2,128,2,16,2,128]{5,4,3,2,1,0:T(2,128)} reshape(f32[2,4096,256]{2,1,0:T(8,128)} %copy.18) | data formatting | bytes 16777216 | tf_op jit(solution)/shard_map/reshape | solution.py:45
  120.9 10.9 %fusion.1 = (f32[2,128,1,16,1,128]{5,4,3,2,1,0:T(1,128)S(1)}, f32[2,128,1,16,1,128]{5,4,3,2,1,0:T(1,128)S(1)}, f32[2,128,1,16,1,128]{5,4,3,2,1,0:T(1,128)S(1)}) fusion(f32[2,128,2,16,2,128]{5,4,3,2,1,0:T(2,128)} %reshape.44), kind=kLoop, calls=%fused_computation.10 | loop fusion | flops 524288 | bytes 14680064 | tf_op jit(solution)/shard_map/slice | solution.py:46
  131.8 0.3 add_bitcast_fusion
  132.1 0.6 pad_maximum_fusion
  132.7 0.5 copy.21
  133.2 5.2 %copy.32 = f32[16,8,64,128]{3,1,2,0:T(8,128)} copy(f32[16,8,64,128]{3,2,1,0:T(8,128)S(1)} %bitcast.34) | data formatting | bytes 8388608
  138.4 0.0 copy-start
  138.4 0.1 reduce-scatter.5.cloned.1.call-update
  138.5 0.6 copy-done
  139.1 0.1 dynamic_slice.3
  139.1 0.1 compare_select_fusion
  139.2 74.3 %reduce-scatter.5.cloned.1.call-done = f32[8,8192]{1,0:T(8,128)} async-done(((f32[128,8192]{1,0:T(8,128)}), f32[8,8192]{1,0:T(8,128)}) %reduce-scatter.5.cloned.1.call-update) | async-done | bytes 262160
  213.5 1.0 copy.27
  214.5 0.7 fusion
  (1 shorter events, 0.0 us)
Async XLA Ops:
  8.8 47.7 %all-to-all-start = ((bf16[16,2,2,4,768]{4,3,2,1,0:T(4,128)(2,1)}), bf16[16,2,2,4,768]{4,3,2,1,0:T(4,128)(2,1)S(1)}, u32[]{:S(2)}, u32[]{:S(2)}) async-start(bf16[16,2,2,4,768]{4,3,2,1,0:T(4,128)(2,1)} %copy.15), calls=%async_computation | async-start | bytes 786432 | tf_op jit(solution)/shard_map/all_to_all | solution.py:30
  32.8 180.7 %reduce-scatter.5.cloned.1.call-start = ((), (), s32[]{:S(2)}) async-start(), calls=%async_computation.3 | async-start | bytes 4456448
  138.4 0.7 copy-start
Sparse Core Ops, SparseCore 0:
  138.6 74.8 reduce-scatter.4
where the time goes:
time: 223 us; the launch traced here: 222 us
  waiting for transfers between devices  97.7 us (44%)
  local copies, waits for them, and re-layouts  29.6 us (13%)
  blocking collectives  29.5 us (13%)
  starting transfers between devices  24 us (11%)
  matrix products  14.7 us (7%)
  between operations  13.5 us (6%)
  other arithmetic  13 us (6%)
    unnamed x2, waiting for transfers between devices  74.3 us
    all_to_all x1, blocking collectives, several_exchanges(): lax.all_to_all(section, axis, split_axis=0, concat_axis=0, tiled=True)  29.5 us
    all_to_all x1, starting transfers between devices, several_exchanges(): lax.all_to_all(section, axis, split_axis=0, concat_axis=0, tiled=True)  24 us
    all_to_all x1, waiting for transfers between devices, several_exchanges(): lax.all_to_all(section, axis, split_axis=0, concat_axis=0, tiled=True)  23.4 us
    dot_general x1, matrix products, contract_block(): jnp.einsum('tkc,tjc->tkj', spinors.reshape(slices, sources * 32, spinors....  14.7 us
    slice x1, other arithmetic, contract_block(): real_part = products[:, :, 0, :, 0, :] + products[:, :, 1, :, 1, :]  10.9 us
    reshape x1, local copies, waits for them, and re-layouts, contract_block(): products = products.reshape(slices, sources, 2, 16, 2, count)  10.8 us
    dot_general x1, local copies, waits for them, and re-layouts, contract_block(): jnp.einsum('tkc,tjc->tkj', spinors.reshape(slices, sources * 32, spinors....  8.91 us
  transfers between devices with their start and end apart: 2, of which 2 were waited for; matrix products, arithmetic and copies ran while one was open for 0% of the time, Pallas kernels for 0%

commit v1 on v0

v1 whole, which is shorter than its diff:
```python
import functools

import jax
import jax.numpy as jnp
from jax import lax
from jax.experimental import pallas as pl
from jax.experimental.pallas import tpu as pltpu
from jax.sharding import PartitionSpec as P

LEVELS = 32766.0
STEPS_PER_OCTAVE = 64.0
LN2 = 0.6931471805599453


def scale_of(code):
    return jnp.exp2(code * (1.0 / STEPS_PER_OCTAVE))


def encode(sums, message_ref, groups, rows):
    largest = jnp.maximum(jnp.max(jnp.abs(sums), axis=1), 1e-30)
    code = jnp.ceil(jnp.log(largest) * (STEPS_PER_OCTAVE / LN2))
    inverse = LEVELS / scale_of(code)
    levels = jnp.round(sums * inverse[:, None, :]).astype(jnp.int32).astype(jnp.int16)
    message_ref[: groups * rows, :] = levels.reshape(groups * rows, levels.shape[2])
    message_ref[groups * rows :, :] = code.astype(jnp.int32).astype(jnp.int16)


def decode(message_ref, groups, rows):
    code = message_ref[groups * rows :, :].astype(jnp.int32).astype(jnp.float32)
    levels = message_ref[: groups * rows, :].astype(jnp.int32).astype(jnp.float32)
    step = scale_of(code) * (1.0 / LEVELS)
    return levels.reshape(groups, rows, levels.shape[1]) * step[:, None, :]


def partial_kernel(owner_ref, spinors_ref, vectors_ref, out_ref):
    slices, sources, rows, sites = spinors_ref.shape
    peers, _, _, own, _ = vectors_ref.shape
    count = peers * own
    half = rows // 2
    for t in range(slices):
        spinors = spinors_ref[t].reshape(sources * rows, sites)
        vectors = jnp.concatenate([vectors_ref[:, t, part].reshape(count, sites) for part in (0, 1)], axis=0)
        products = lax.dot_general(
            spinors, vectors, (((1,), (1,)), ((), ())), preferred_element_type=jnp.float32
        ).reshape(sources, rows, 2 * count)
        real_re = products[:, :half, :count]
        imag_re = products[:, half:, :count]
        real_im = products[:, :half, count:]
        imag_im = products[:, half:, count:]
        out_ref[0, t * sources : (t + 1) * sources, :half, :] = real_re + imag_im
        out_ref[0, t * sources : (t + 1) * sources, half:, :] = imag_re - real_im


def partials(owners, solutions, vectors, sources):
    slices, _, rows, sites = solutions.shape
    count = vectors.shape[0] * vectors.shape[3]
    return pl.pallas_call(
        partial_kernel,
        grid_spec=pltpu.PrefetchScalarGridSpec(
            num_scalar_prefetch=1,
            grid=(owners.shape[0],),
            in_specs=[
                pl.BlockSpec((slices, sources, rows, sites), lambda i, who: (0, who[i], 0, 0)),
                pl.BlockSpec(memory_space=pltpu.VMEM),
            ],
            out_specs=pl.BlockSpec((1, slices * sources, rows, count), lambda i, who: (i, 0, 0, 0)),
        ),
        out_shape=pltpu.VMEM((owners.shape[0], slices * sources, rows, count), jnp.float32),
        cost_estimate=pl.CostEstimate(
            flops=owners.shape[0] * slices * sources * rows * sites * 2 * count * 2,
            bytes_accessed=owners.shape[0] * slices * sources * (rows * sites * 2 + rows * count * 4),
            transcendentals=0,
        ),
    )(owners, solutions, in_vmem(vectors))


def step_kernel(own_ref, *refs, received):
    arms = len(received)
    _, groups, rows, _ = own_ref.shape
    messages, outs = refs[: sum(received)], refs[sum(received) :]
    taken = 0
    for arm in range(arms):
        sums = own_ref[arm]
        if received[arm]:
            sums = sums + decode(messages[taken], groups, rows)
            taken += 1
        encode(sums, outs[arm], groups, rows)


def step(own, messages):
    _, groups, rows, count = own.shape
    arms = len(messages)
    arrived = [m for m in messages if m is not None]
    shape = pltpu.VMEM((groups * (rows + 1), count), jnp.int16)
    return pl.pallas_call(
        functools.partial(step_kernel, received=tuple(m is not None for m in messages)),
        out_shape=[shape] * arms,
        in_specs=[pl.BlockSpec(memory_space=pltpu.VMEM)] * (1 + len(arrived)),
        out_specs=[pl.BlockSpec(memory_space=pltpu.VMEM)] * arms,
    )(in_vmem(own), *map(in_vmem, arrived))


def last_kernel(own_ref, left_ref, right_ref, signs_ref, out_ref):
    _, groups, rows, count = own_ref.shape
    sums = own_ref[0] + decode(left_ref, groups, rows) + decode(right_ref, groups, rows)
    signed = sums * signs_ref[...][:, None, :]
    out_ref[...] = signed.astype(jnp.bfloat16).reshape(out_ref.shape)


def last(own, left, right, signs, slices):
    _, groups, rows, count = own.shape
    return pl.pallas_call(
        last_kernel,
        out_shape=jax.ShapeDtypeStruct((slices, groups // slices, rows, count), jnp.bfloat16),
        in_specs=[pl.BlockSpec(memory_space=pltpu.VMEM)] * 4,
        out_specs=pl.BlockSpec(memory_space=pltpu.VMEM),
    )(in_vmem(own), in_vmem(left), in_vmem(right), in_vmem(signs))


def exchange(eigvecs, devices):
    slices, parts, own, whole = eigvecs.shape
    pieces = jnp.moveaxis(eigvecs.reshape(slices, parts, own, devices, whole // devices), 3, 0)
    return lax.all_to_all(pieces, "space", split_axis=0, concat_axis=0, tiled=True)


def in_vmem(array):
    return pltpu.with_memory_space_constraint(array, pltpu.VMEM)


def shards(solutions, eigvecs, source_time):
    slices = solutions.shape[0]
    devices = lax.axis_size("space")
    sources = solutions.shape[1] // devices
    count = eigvecs.shape[2] * devices
    me = lax.axis_index("space")
    vectors = exchange(eigvecs, devices)

    owned_times = lax.dynamic_slice_in_dim(source_time, me * sources, sources)
    slice_index = lax.axis_index("tm") * slices + jnp.arange(slices, dtype=jnp.int32)
    signs = jnp.where(slice_index[:, None] < owned_times[None, :], -1.0, 1.0).astype(jnp.float32)
    signs = jnp.broadcast_to(signs.reshape(slices * sources, 1), (slices * sources, count))

    ahead = [(i, (i + 1) % devices) for i in range(devices)]
    back = [(i, (i - 1) % devices) for i in range(devices)]
    reach = devices // 2
    offsets = jnp.array([reach] + [s * d for d in range(reach - 1, 0, -1) for s in (1, -1)] + [0], jnp.int32)
    owners = (me + offsets) % devices

    own = partials(owners[:1], solutions, vectors, sources)
    (right,) = step(own, [None])
    right = lax.ppermute(right, "space", ahead)
    left = None
    for k in range(1, reach):
        own = partials(owners[2 * k - 1 : 2 * k + 1], solutions, vectors, sources)
        right, left = step(own, [right, left])
        right = lax.ppermute(right, "space", ahead)
        left = lax.ppermute(left, "space", back)
    own = partials(owners[2 * reach - 1 :], solutions, vectors, sources)
    return last(own, right, left, signs, slices)


def solution(mesh):
    return jax.shard_map(
        shards,
        mesh=mesh,
        in_specs=(
            P(("cfg", "tm"), None, None, "space"),
            P(("cfg", "tm"), None, "space", None),
            P("cfg"),
        ),
        out_specs=P(("cfg", "tm"), "space", None, None),
        check_vma=False,
    )
```

time: 223 us -> 128 us (0.57)
  waiting for transfers between devices: 97.7 us -> 48.8 us
  blocking collectives: 29.5 us -> 0 us
  local copies, waits for them, and re-layouts: 29.6 us -> 3.63 us
  Pallas kernels: 0 us -> 25.5 us
  starting transfers between devices: 24 us -> 48.7 us
  matrix products: 14.7 us -> 0 us
  between operations: 13.5 us -> 0.17 us
  other arithmetic: 13 us -> 0.74 us
    unnamed x2 -> x0, waiting for transfers between devices: 74.3 us -> none
    all_to_all x1 -> x0, blocking collectives: 29.5 us -> none  [several_exchanges(): lax.all_to_all(section, axis, split_axis=0, concat_axis=0, tiled=True)]
    pallas_call x0 -> x18, Pallas kernels: none -> 25.5 us  [the longest x9 23 us: partials(): pl.pallas_call(partial_kernel, grid_spec=pltpu.PrefetchScalarGridSpec(num...]
    ppermute x0 -> x15, starting transfers between devices: none -> 24.8 us  [the longest x7 21.3 us: shards(): left = lax.ppermute(left, 'space', back)]
    dot_general x1 -> x0, matrix products: 14.7 us -> none  [contract_block(): jnp.einsum('tkc,tjc->tkj', spinors.reshape(slices, sources * 32, spinors....]
    all_to_all x1, waiting for transfers between devices: 23.4 us -> 37.6 us  [exchange(): lax.all_to_all(pieces, 'space', split_axis=0, concat_axis=0, tiled=True)]
    ppermute x0 -> x15, waiting for transfers between devices: none -> 11.2 us  [the longest x8 10.1 us: shards(): right = lax.ppermute(right, 'space', ahead)]
    slice x1 -> x0, other arithmetic: 10.9 us -> none  [contract_block(): real_part = products[:, :, 0, :, 0, :] + products[:, :, 1, :, 1, :]]
  transfers between devices with their start and end apart: 2 -> 16, of which waited for: 2 -> 10; matrix products, arithmetic and copies ran while one was open for 0% -> 2% of each run, Pallas kernels for 0% -> 16%
where the time goes in v1:
time: 128 us
  waiting for transfers between devices  48.8 us (38%)
  starting transfers between devices  48.7 us (38%)
  Pallas kernels  25.5 us (20%)
  local copies, waits for them, and re-layouts  3.63 us (3%)
    all_to_all x1, waiting for transfers between devices, exchange(): lax.all_to_all(pieces, 'space', split_axis=0, concat_axis=0, tiled=True)  37.6 us
    all_to_all x1, starting transfers between devices, exchange(): lax.all_to_all(pieces, 'space', split_axis=0, concat_axis=0, tiled=True)  24 us
    pallas_call x9, Pallas kernels, partials(): pl.pallas_call(partial_kernel, grid_spec=pltpu.PrefetchScalarGridSpec(num...  23 us
    ppermute x7, starting transfers between devices, shards(): left = lax.ppermute(left, 'space', back)  21.3 us
    ppermute x8, waiting for transfers between devices, shards(): right = lax.ppermute(right, 'space', ahead)  10.1 us
    ppermute x8, starting transfers between devices, shards(): right = lax.ppermute(right, 'space', ahead)  3.46 us
  transfers between devices with their start and end apart: 16, of which 10 were waited for; matrix products, arithmetic and copies ran while one was open for 2% of the time, Pallas kernels for 16%

profile of v1, /device:TPU:34, one launch (start us, length us, event | category | flops | bytes accessed | tf_op | source)
XLA Modules:
  0.0 127.7 jit_solution(8488917846643707252)
XLA Ops:
  0.0 2.1 %copy.8 = bf16[2,2,1,16,8,768]{5,4,2,1,0,3:T(8,128)(2,1)} copy(bf16[2,2,1,16,8,768]{5,4,3,2,1,0:T(8,128)(2,1)} %bitcast.7) | data formatting | bytes 1572864 | tf_op jit(solution)/shard_map/reshape | solution.py:122
  2.1 24.0 %all-to-all-start = ((bf16[16,2,2,8,768]{4,3,2,1,0:T(8,128)(2,1)}), bf16[16,2,2,8,768]{4,3,2,1,0:T(8,128)(2,1)S(1)}, u32[]{:S(2)}, u32[]{:S(2)}) async-start(bf16[16,2,2,8,768]{4,3,2,1,0:T(8,128)(2,1)} %bitcast.6), calls=%async_computation | async-start | bytes 1572864 | tf_op jit(solution)/shard_map/all_to_all | solution.py:123
  26.1 0.7 and_select_fusion
  26.8 0.6 fusion.1
  27.4 37.6 %all-to-all-done.vectors_ref = bf16[16,2,2,8,768]{4,3,2,1,0:T(8,128)(2,1)S(1)} async-done(((bf16[16,2,2,8,768]{4,3,2,1,0:T(8,128)(2,1)}), bf16[16,2,2,8,768]{4,3,2,1,0:T(8,128)(2,1)S(1)}, u32[]{:S(2)}, u32[]{:S(2)}) %all-to-all-start) | async-done | bytes 786464 | tf_op jit(solution)/shard_map/all_to_all | solution.py:123
  65.0 2.2 %shard_map.54.own_ref = f32[1,16,32,128]{3,2,1,0:T(8,128)S(1)} custom-call(s32[1]{0:T(128)} %get-tuple-element.33.owner_ref, bf16[2,128,32,768]{3,2,1,0:T(8,128)(2,1)} %spinors_ref.17, bf16[16,2,2,8,768]{4,3,2,1,0:T(8,128)(2,1)S(1)} %all-to-all-done.vectors_ref), custom_call_target="tpu_custom_call" | custom-call | flops 201326592 | bytes 1048576 | tf_op jit(solution)/shard_map/pallas_call | solution.py:57
  67.2 0.1 shard_map.55
  67.3 2.2 %collective-permute-start = (s16[528,128]{1,0:T(8,128)(2,1)S(1)}, s16[528,128]{1,0:T(8,128)(2,1)S(1)}, u32[]{:S(2)}, u32[]{:S(2)}) collective-permute-start(s16[528,128]{1,0:T(8,128)(2,1)S(1)} %shard_map.55), channel_id=1, source_target_pairs={{0,8},{8,16},{16,24},{24,32},{32,40},{40,48},{48,56},{56,64},{64,7... | collective-permute-start | bytes 405512 | tf_op jit(solution)/shard_map/ppermute | solution.py:151
  69.4 0.7 fusion.2
  70.1 2.6 %shard_map.53.own_ref = f32[2,16,32,128]{3,2,1,0:T(8,128)S(1)} custom-call(s32[2]{0:T(128)} %get-tuple-element.35.owner_ref, bf16[2,128,32,768]{3,2,1,0:T(8,128)(2,1)} %spinors_ref.17, bf16[16,2,2,8,768]{4,3,2,1,0:T(8,128)(2,1)S(1)} %all-to-all-done.vectors_ref), custom_call_target="tpu_custom_call" | custom-call | flops 402653184 | bytes 2097152 | tf_op jit(solution)/shard_map/pallas_call | solution.py:57
  72.8 4.2 %collective-permute-done.refs_0_ = s16[528,128]{1,0:T(8,128)(2,1)S(1)} collective-permute-done((s16[528,128]{1,0:T(8,128)(2,1)S(1)}, s16[528,128]{1,0:T(8,128)(2,1)S(1)}, u32[]{:S(2)}, u32[]{:S(2)}) %collective-permute-start) | collective-permute-done | bytes 135200 | tf_op jit(solution)/shard_map/ppermute | solution.py:151
  77.0 0.2 shard_map.56
  77.2 0.1 collective-permute-start.1
  77.3 3.2 %collective-permute-start.2 = (s16[528,128]{1,0:T(8,128)(2,1)S(1)}, s16[528,128]{1,0:T(8,128)(2,1)S(1)}, u32[]{:S(2)}, u32[]{:S(2)}) collective-permute-start(s16[528,128]{1,0:T(8,128)(2,1)S(1)} %get-tuple-element.20), channel_id=1, source_target_pairs={{0,120},{8,0},{16,8},{24,16},{32,24},{40,32},{48,40},{56,48},{64,5... | collective-permute-start | bytes 405512 | tf_op jit(solution)/shard_map/ppermute | solution.py:157
  80.6 2.6 %shard_map.52.own_ref = f32[2,16,32,128]{3,2,1,0:T(8,128)S(1)} custom-call(s32[2]{0:T(128)} %get-tuple-element.36.owner_ref, bf16[2,128,32,768]{3,2,1,0:T(8,128)(2,1)} %spinors_ref.17, bf16[16,2,2,8,768]{4,3,2,1,0:T(8,128)(2,1)S(1)} %all-to-all-done.vectors_ref), custom_call_target="tpu_custom_call" | custom-call | flops 402653184 | bytes 2097152 | tf_op jit(solution)/shard_map/pallas_call | solution.py:57
  83.2 0.6 collective-permute-done.1.refs_0_
  83.8 0.0 collective-permute-done.2.refs_1_
  83.8 0.2 shard_map.57
  84.0 0.1 collective-permute-start.3
  84.2 3.2 %collective-permute-start.4 = (s16[528,128]{1,0:T(8,128)(2,1)S(1)}, s16[528,128]{1,0:T(8,128)(2,1)S(1)}, u32[]{:S(2)}, u32[]{:S(2)}) collective-permute-start(s16[528,128]{1,0:T(8,128)(2,1)S(1)} %get-tuple-element.22), channel_id=1, source_target_pairs={{0,120},{8,0},{16,8},{24,16},{32,24},{40,32},{48,40},{56,48},{64,5... | collective-permute-start | bytes 405512 | tf_op jit(solution)/shard_map/ppermute | solution.py:157
  87.4 2.6 %shard_map.51.own_ref = f32[2,16,32,128]{3,2,1,0:T(8,128)S(1)} custom-call(s32[2]{0:T(128)} %get-tuple-element.37.owner_ref, bf16[2,128,32,768]{3,2,1,0:T(8,128)(2,1)} %spinors_ref.17, bf16[16,2,2,8,768]{4,3,2,1,0:T(8,128)(2,1)S(1)} %all-to-all-done.vectors_ref), custom_call_target="tpu_custom_call" | custom-call | flops 402653184 | bytes 2097152 | tf_op jit(solution)/shard_map/pallas_call | solution.py:57
  90.0 0.3 collective-permute-done.3.refs_0_
  90.4 0.0 collective-permute-done.4.refs_1_
  90.4 0.2 shard_map.58
  90.6 0.4 collective-permute-start.5
  91.0 3.1 %collective-permute-start.6 = (s16[528,128]{1,0:T(8,128)(2,1)S(1)}, s16[528,128]{1,0:T(8,128)(2,1)S(1)}, u32[]{:S(2)}, u32[]{:S(2)}) collective-permute-start(s16[528,128]{1,0:T(8,128)(2,1)S(1)} %get-tuple-element.24), channel_id=1, source_target_pairs={{0,120},{8,0},{16,8},{24,16},{32,24},{40,32},{48,40},{56,48},{64,5... | collective-permute-start | bytes 405512 | tf_op jit(solution)/shard_map/ppermute | solution.py:157
  94.1 0.0 copy-start
  94.1 2.8 %shard_map.50.own_ref = f32[2,16,32,128]{3,2,1,0:T(8,128)S(1)} custom-call(s32[2]{0:T(128)} %get-tuple-element.38.owner_ref, bf16[2,128,32,768]{3,2,1,0:T(8,128)(2,1)} %spinors_ref.17, bf16[16,2,2,8,768]{4,3,2,1,0:T(8,128)(2,1)S(1)} %all-to-all-done.vectors_ref), custom_call_target="tpu_custom_call" | custom-call | flops 402653184 | bytes 2097152 | tf_op jit(solution)/shard_map/pallas_call | solution.py:57
  96.9 0.2 collective-permute-done.5.refs_0_
  97.1 0.0 collective-permute-done.6.refs_1_
  97.1 0.2 shard_map.59
  97.3 0.4 collective-permute-start.7
  97.7 3.1 %collective-permute-start.8 = (s16[528,128]{1,0:T(8,128)(2,1)S(1)}, s16[528,128]{1,0:T(8,128)(2,1)S(1)}, u32[]{:S(2)}, u32[]{:S(2)}) collective-permute-start(s16[528,128]{1,0:T(8,128)(2,1)S(1)} %get-tuple-element.26), channel_id=1, source_target_pairs={{0,120},{8,0},{16,8},{24,16},{32,24},{40,32},{48,40},{56,48},{64,5... | collective-permute-start | bytes 405512 | tf_op jit(solution)/shard_map/ppermute | solution.py:157
  100.8 2.6 %shard_map.49.own_ref = f32[2,16,32,128]{3,2,1,0:T(8,128)S(1)} custom-call(s32[2]{0:T(128)} %get-tuple-element.39.owner_ref, bf16[2,128,32,768]{3,2,1,0:T(8,128)(2,1)} %spinors_ref.17, bf16[16,2,2,8,768]{4,3,2,1,0:T(8,128)(2,1)S(1)} %all-to-all-done.vectors_ref), custom_call_target="tpu_custom_call" | custom-call | flops 402653184 | bytes 2097152 | tf_op jit(solution)/shard_map/pallas_call | solution.py:57
  103.5 1.6 %collective-permute-done.7.refs_0_ = s16[528,128]{1,0:T(8,128)(2,1)S(1)} collective-permute-done((s16[528,128]{1,0:T(8,128)(2,1)S(1)}, s16[528,128]{1,0:T(8,128)(2,1)S(1)}, u32[]{:S(2)}, u32[]{:S(2)}) %collective-permute-start.7) | collective-permute-done | bytes 135200 | tf_op jit(solution)/shard_map/ppermute | solution.py:156
  105.1 0.0 collective-permute-done.8.refs_1_
  105.1 0.2 shard_map.60
  105.3 2.1 %collective-permute-start.10 = (s16[528,128]{1,0:T(8,128)(2,1)S(1)}, s16[528,128]{1,0:T(8,128)(2,1)S(1)}, u32[]{:S(2)}, u32[]{:S(2)}) collective-permute-start(s16[528,128]{1,0:T(8,128)(2,1)S(1)} %get-tuple-element.28), channel_id=1, source_target_pairs={{0,120},{8,0},{16,8},{24,16},{32,24},{40,32},{48,40},{56,48},{64,5... | collective-permute-start | bytes 405512 | tf_op jit(solution)/shard_map/ppermute | solution.py:157
  107.4 0.1 collective-permute-start.9
  107.5 0.0 copy-done
  107.5 0.1 dynamic_slice.3
  107.5 2.6 %shard_map.48.own_ref = f32[2,16,32,128]{3,2,1,0:T(8,128)S(1)} custom-call(s32[2]{0:T(128)} %get-tuple-element.40.owner_ref, bf16[2,128,32,768]{3,2,1,0:T(8,128)(2,1)} %spinors_ref.17, bf16[16,2,2,8,768]{4,3,2,1,0:T(8,128)(2,1)S(1)} %all-to-all-done.vectors_ref), custom_call_target="tpu_custom_call" | custom-call | flops 402653184 | bytes 2097152 | tf_op jit(solution)/shard_map/pallas_call | solution.py:57
  110.2 1.1 collective-permute-done.10.refs_1_
  111.3 2.4 %collective-permute-done.9.refs_0_ = s16[528,128]{1,0:T(8,128)(2,1)S(1)} collective-permute-done((s16[528,128]{1,0:T(8,128)(2,1)S(1)}, s16[528,128]{1,0:T(8,128)(2,1)S(1)}, u32[]{:S(2)}, u32[]{:S(2)}) %collective-permute-start.9) | collective-permute-done | bytes 135200 | tf_op jit(solution)/shard_map/ppermute | solution.py:156
  113.6 0.2 shard_map.61
  113.9 0.1 collective-permute-start.11
  114.0 3.2 %collective-permute-start.12 = (s16[528,128]{1,0:T(8,128)(2,1)S(1)}, s16[528,128]{1,0:T(8,128)(2,1)S(1)}, u32[]{:S(2)}, u32[]{:S(2)}) collective-permute-start(s16[528,128]{1,0:T(8,128)(2,1)S(1)} %get-tuple-element.30), channel_id=1, source_target_pairs={{0,120},{8,0},{16,8},{24,16},{32,24},{40,32},{48,40},{56,48},{64,5... | collective-permute-start | bytes 405512 | tf_op jit(solution)/shard_map/ppermute | solution.py:157
  117.2 2.6 %shard_map.47.own_ref = f32[2,16,32,128]{3,2,1,0:T(8,128)S(1)} custom-call(s32[2]{0:T(128)} %get-tuple-element.41.owner_ref, bf16[2,128,32,768]{3,2,1,0:T(8,128)(2,1)} %spinors_ref.17, bf16[16,2,2,8,768]{4,3,2,1,0:T(8,128)(2,1)S(1)} %all-to-all-done.vectors_ref), custom_call_target="tpu_custom_call" | custom-call | flops 402653184 | bytes 2097152 | tf_op jit(solution)/shard_map/pallas_call | solution.py:57
  119.9 0.3 collective-permute-done.11.refs_0_
  120.2 0.0 collective-permute-done.12.refs_1_
  120.2 0.2 shard_map.62
  120.5 0.1 collective-permute-start.13
  120.6 3.3 %collective-permute-start.14 = (s16[528,128]{1,0:T(8,128)(2,1)S(1)}, s16[528,128]{1,0:T(8,128)(2,1)S(1)}, u32[]{:S(2)}, u32[]{:S(2)}) collective-permute-start(s16[528,128]{1,0:T(8,128)(2,1)S(1)} %get-tuple-element.32), channel_id=1, source_target_pairs={{0,120},{8,0},{16,8},{24,16},{32,24},{40,32},{48,40},{56,48},{64,5... | collective-permute-start | bytes 405512 | tf_op jit(solution)/shard_map/ppermute | solution.py:157
  124.0 0.1 compare_select_fusion.2
  124.0 0.1 select_n.24
  124.1 2.2 %shard_map.46.own_ref = f32[1,16,32,128]{3,2,1,0:T(8,128)S(1)} custom-call(s32[1]{0:T(128)} %get-tuple-element.34.owner_ref, bf16[2,128,32,768]{3,2,1,0:T(8,128)(2,1)} %spinors_ref.17, bf16[16,2,2,8,768]{4,3,2,1,0:T(8,128)(2,1)S(1)} %all-to-all-done.vectors_ref), custom_call_target="tpu_custom_call" | custom-call | flops 201326592 | bytes 1048576 | tf_op jit(solution)/shard_map/pallas_call | solution.py:57
  126.3 0.5 collective-permute-done.13.left_ref
  126.8 0.0 collective-permute-done.14.right_ref
  126.8 0.1 broadcast_in_dim.17.signs_ref
  126.9 0.8 shard_map.63
  (1 shorter events, 0.0 us)
Async XLA Ops:
  2.1 62.9 %all-to-all-start = ((bf16[16,2,2,8,768]{4,3,2,1,0:T(8,128)(2,1)}), bf16[16,2,2,8,768]{4,3,2,1,0:T(8,128)(2,1)S(1)}, u32[]{:S(2)}, u32[]{:S(2)}) async-start(bf16[16,2,2,8,768]{4,3,2,1,0:T(8,128)(2,1)} %bitcast.6), calls=%async_computation | async-start | bytes 1572864 | tf_op jit(solution)/shard_map/all_to_all | solution.py:123
  67.3 9.7 %collective-permute-start = (s16[528,128]{1,0:T(8,128)(2,1)S(1)}, s16[528,128]{1,0:T(8,128)(2,1)S(1)}, u32[]{:S(2)}, u32[]{:S(2)}) collective-permute-start(s16[528,128]{1,0:T(8,128)(2,1)S(1)} %shard_map.55), channel_id=1, source_target_pairs={{0,8},{8,16},{16,24},{24,32},{32,40},{40,48},{48,56},{56,64},{64,7... | collective-permute-start | bytes 405512 | tf_op jit(solution)/shard_map/ppermute | solution.py:151
  77.2 6.6 %collective-permute-start.1 = (s16[528,128]{1,0:T(8,128)(2,1)S(1)}, s16[528,128]{1,0:T(8,128)(2,1)S(1)}, u32[]{:S(2)}, u32[]{:S(2)}) collective-permute-start(s16[528,128]{1,0:T(8,128)(2,1)S(1)} %get-tuple-element.19), channel_id=1, source_target_pairs={{0,8},{8,16},{16,24},{24,32},{32,40},{40,48},{48,56},{56,64},{64,7... | collective-permute-start | bytes 405512 | tf_op jit(solution)/shard_map/ppermute | solution.py:156
  77.3 6.4 %collective-permute-start.2 = (s16[528,128]{1,0:T(8,128)(2,1)S(1)}, s16[528,128]{1,0:T(8,128)(2,1)S(1)}, u32[]{:S(2)}, u32[]{:S(2)}) collective-permute-start(s16[528,128]{1,0:T(8,128)(2,1)S(1)} %get-tuple-element.20), channel_id=1, source_target_pairs={{0,120},{8,0},{16,8},{24,16},{32,24},{40,32},{48,40},{56,48},{64,5... | collective-permute-start | bytes 405512 | tf_op jit(solution)/shard_map/ppermute | solution.py:157
  84.0 6.3 %collective-permute-start.3 = (s16[528,128]{1,0:T(8,128)(2,1)S(1)}, s16[528,128]{1,0:T(8,128)(2,1)S(1)}, u32[]{:S(2)}, u32[]{:S(2)}) collective-permute-start(s16[528,128]{1,0:T(8,128)(2,1)S(1)} %get-tuple-element.21), channel_id=1, source_target_pairs={{0,8},{8,16},{16,24},{24,32},{32,40},{40,48},{48,56},{56,64},{64,7... | collective-permute-start | bytes 405512 | tf_op jit(solution)/shard_map/ppermute | solution.py:156
  84.2 6.2 %collective-permute-start.4 = (s16[528,128]{1,0:T(8,128)(2,1)S(1)}, s16[528,128]{1,0:T(8,128)(2,1)S(1)}, u32[]{:S(2)}, u32[]{:S(2)}) collective-permute-start(s16[528,128]{1,0:T(8,128)(2,1)S(1)} %get-tuple-element.22), channel_id=1, source_target_pairs={{0,120},{8,0},{16,8},{24,16},{32,24},{40,32},{48,40},{56,48},{64,5... | collective-permute-start | bytes 405512 | tf_op jit(solution)/shard_map/ppermute | solution.py:157
  90.6 6.5 %collective-permute-start.5 = (s16[528,128]{1,0:T(8,128)(2,1)S(1)}, s16[528,128]{1,0:T(8,128)(2,1)S(1)}, u32[]{:S(2)}, u32[]{:S(2)}) collective-permute-start(s16[528,128]{1,0:T(8,128)(2,1)S(1)} %get-tuple-element.23), channel_id=1, source_target_pairs={{0,8},{8,16},{16,24},{24,32},{32,40},{40,48},{48,56},{56,64},{64,7... | collective-permute-start | bytes 405512 | tf_op jit(solution)/shard_map/ppermute | solution.py:156
  91.0 6.1 %collective-permute-start.6 = (s16[528,128]{1,0:T(8,128)(2,1)S(1)}, s16[528,128]{1,0:T(8,128)(2,1)S(1)}, u32[]{:S(2)}, u32[]{:S(2)}) collective-permute-start(s16[528,128]{1,0:T(8,128)(2,1)S(1)} %get-tuple-element.24), channel_id=1, source_target_pairs={{0,120},{8,0},{16,8},{24,16},{32,24},{40,32},{48,40},{56,48},{64,5... | collective-permute-start | bytes 405512 | tf_op jit(solution)/shard_map/ppermute | solution.py:157
  94.1 13.4 %copy-start = (s32[128]{0:T(128)S(1)}, s32[128]{0:T(128)}, u32[]{:S(2)}) copy-start(s32[128]{0:T(128)} %param.6) | copy-start | bytes 1540
  97.3 7.7 %collective-permute-start.7 = (s16[528,128]{1,0:T(8,128)(2,1)S(1)}, s16[528,128]{1,0:T(8,128)(2,1)S(1)}, u32[]{:S(2)}, u32[]{:S(2)}) collective-permute-start(s16[528,128]{1,0:T(8,128)(2,1)S(1)} %get-tuple-element.25), channel_id=1, source_target_pairs={{0,8},{8,16},{16,24},{24,32},{32,40},{40,48},{48,56},{56,64},{64,7... | collective-permute-start | bytes 405512 | tf_op jit(solution)/shard_map/ppermute | solution.py:156
  97.7 7.4 %collective-permute-start.8 = (s16[528,128]{1,0:T(8,128)(2,1)S(1)}, s16[528,128]{1,0:T(8,128)(2,1)S(1)}, u32[]{:S(2)}, u32[]{:S(2)}) collective-permute-start(s16[528,128]{1,0:T(8,128)(2,1)S(1)} %get-tuple-element.26), channel_id=1, source_target_pairs={{0,120},{8,0},{16,8},{24,16},{32,24},{40,32},{48,40},{56,48},{64,5... | collective-permute-start | bytes 405512 | tf_op jit(solution)/shard_map/ppermute | solution.py:157
  105.3 5.9 %collective-permute-start.10 = (s16[528,128]{1,0:T(8,128)(2,1)S(1)}, s16[528,128]{1,0:T(8,128)(2,1)S(1)}, u32[]{:S(2)}, u32[]{:S(2)}) collective-permute-start(s16[528,128]{1,0:T(8,128)(2,1)S(1)} %get-tuple-element.28), channel_id=1, source_target_pairs={{0,120},{8,0},{16,8},{24,16},{32,24},{40,32},{48,40},{56,48},{64,5... | collective-permute-start | bytes 405512 | tf_op jit(solution)/shard_map/ppermute | solution.py:157
  107.4 6.2 %collective-permute-start.9 = (s16[528,128]{1,0:T(8,128)(2,1)S(1)}, s16[528,128]{1,0:T(8,128)(2,1)S(1)}, u32[]{:S(2)}, u32[]{:S(2)}) collective-permute-start(s16[528,128]{1,0:T(8,128)(2,1)S(1)} %get-tuple-element.27), channel_id=1, source_target_pairs={{0,8},{8,16},{16,24},{24,32},{32,40},{40,48},{48,56},{56,64},{64,7... | collective-permute-start | bytes 405512 | tf_op jit(solution)/shard_map/ppermute | solution.py:156
  113.9 6.3 %collective-permute-start.11 = (s16[528,128]{1,0:T(8,128)(2,1)S(1)}, s16[528,128]{1,0:T(8,128)(2,1)S(1)}, u32[]{:S(2)}, u32[]{:S(2)}) collective-permute-start(s16[528,128]{1,0:T(8,128)(2,1)S(1)} %get-tuple-element.29), channel_id=1, source_target_pairs={{0,8},{8,16},{16,24},{24,32},{32,40},{40,48},{48,56},{56,64},{64,7... | collective-permute-start | bytes 405512 | tf_op jit(solution)/shard_map/ppermute | solution.py:156
  114.0 6.2 %collective-permute-start.12 = (s16[528,128]{1,0:T(8,128)(2,1)S(1)}, s16[528,128]{1,0:T(8,128)(2,1)S(1)}, u32[]{:S(2)}, u32[]{:S(2)}) collective-permute-start(s16[528,128]{1,0:T(8,128)(2,1)S(1)} %get-tuple-element.30), channel_id=1, source_target_pairs={{0,120},{8,0},{16,8},{24,16},{32,24},{40,32},{48,40},{56,48},{64,5... | collective-permute-start | bytes 405512 | tf_op jit(solution)/shard_map/ppermute | solution.py:157
  120.5 6.3 %collective-permute-start.13 = (s16[528,128]{1,0:T(8,128)(2,1)S(1)}, s16[528,128]{1,0:T(8,128)(2,1)S(1)}, u32[]{:S(2)}, u32[]{:S(2)}) collective-permute-start(s16[528,128]{1,0:T(8,128)(2,1)S(1)} %get-tuple-element.31), channel_id=1, source_target_pairs={{0,8},{8,16},{16,24},{24,32},{32,40},{40,48},{48,56},{56,64},{64,7... | collective-permute-start | bytes 405512 | tf_op jit(solution)/shard_map/ppermute | solution.py:156
  120.6 6.2 %collective-permute-start.14 = (s16[528,128]{1,0:T(8,128)(2,1)S(1)}, s16[528,128]{1,0:T(8,128)(2,1)S(1)}, u32[]{:S(2)}, u32[]{:S(2)}) collective-permute-start(s16[528,128]{1,0:T(8,128)(2,1)S(1)} %get-tuple-element.32), channel_id=1, source_target_pairs={{0,120},{8,0},{16,8},{24,16},{32,24},{40,32},{48,40},{56,48},{64,5... | collective-permute-start | bytes 405512 | tf_op jit(solution)/shard_map/ppermute | solution.py:157
